TPU v7x, 128 devices: a whole 4x4x4 slice. The times are simulated.
128 devices in a mesh: seq: 16 (over x_lo, y, core), hid: 8 (over x_hi, z).
Axes of the slice: x: 4 (x_hi: 2, x_lo: 2; x = x_hi * 2 + x_lo), y: 4, z: 4, core: 2. Of those that a mesh axis runs over, the one named last changes fastest.
Arguments:
- hidden: bfloat16 [8192, 4096], P('seq', 'hid'), may hold values from -6 to 6
- w_in: bfloat16 [2, 4096, 1024], P(None, 'hid'), may hold values from -0.09863281 to 0.09863281
- embedding: bfloat16 [1, 2048, 1024], replicated, may hold values from -6 to 6
- depth_gain: float32 [2, 1024], replicated, may hold values from 0.25 to 1.75
- w_out: bfloat16 [1024, 2, 2048], P(('seq', 'hid')), may hold values from -0.43554688 to 0.43554688
- codebook_ids: int32 [2, 8192], P(None, ('seq', 'hid')), may hold values from 0 to 2047
Outputs:
- grad_hidden: bfloat16 [8192, 4096], P('seq', 'hid')
- grad_in: float32 [2, 4096, 1024], P(None, 'hid', 'seq')
- grad_out: float32 [1024, 2, 2048], P(('seq', 'hid'))
All inputs are finite; a program needn't handle non-finite values.
Results may differ from a plain program's by a relative error of at most 0.01.
Values may be sent and summed in bfloat16 or wider, within the bound.
A program may use at most 128 MiB of HBM per device.

v0:
```python
import jax
import jax.numpy as jnp
from jax import lax
from jax.sharding import PartitionSpec as P


def shards(hidden, w_in, embedding, depth_gain, w_out, codebook_ids):
    hid_count = lax.axis_size("hid")
    seq_count = lax.axis_size("seq")
    width_in = hidden.shape[1] * hid_count
    steps = w_in.shape[0]
    depth = w_in.shape[2]
    entries = w_out.shape[2]
    group_rows = hidden.shape[0]
    hidden_f = hidden.astype(jnp.float32)
    square_part = jnp.sum(hidden_f * hidden_f, axis=1)
    proj_part = jnp.einsum("fd,kde->fke", hidden, w_in, preferred_element_type=jnp.float32)
    proj_flat, squares = (
        lax.psum_scatter(
            proj_part.reshape(group_rows, steps * depth), "hid", scatter_dimension=0, tiled=True
        ),
        lax.psum_scatter(square_part, "hid", scatter_dimension=0, tiled=True),
    )
    owned = proj_flat.shape[0]
    proj = proj_flat.reshape(owned, steps, depth)
    ratio = lax.rsqrt(squares / width_in + 1e-06)
    pieces = [jnp.zeros((owned, depth), jnp.float32)]
    pieces.append(jnp.take(embedding[0], codebook_ids[0], axis=0).astype(jnp.float32))
    x_rows = ratio[:, None, None] * proj + jnp.stack(pieces, axis=1)
    scale = lax.rsqrt(jnp.mean(x_rows * x_rows, axis=2, keepdims=True) + 1e-06)
    normed = (x_rows * scale * depth_gain[None]).astype(jnp.bfloat16)
    full_head = lax.all_gather(w_out, ("seq", "hid"), axis=0, tiled=True)
    logits = jnp.einsum("fkd,dkc->fkc", normed, full_head, preferred_element_type=jnp.float32)
    targets = codebook_ids.T
    lse = jax.nn.logsumexp(logits, axis=2)
    onehot = (targets[:, :, None] == jnp.arange(entries, dtype=jnp.int32)[None, None, :]).astype(
        jnp.float32
    )
    loss_weight = 2.0 * entries / (owned * seq_count * hid_count)
    d_logit = ((jnp.exp(logits - lse[:, :, None]) - onehot) * loss_weight).astype(jnp.bfloat16)
    grad_out = lax.psum_scatter(
        jnp.einsum("fkd,fkc->dkc", normed, d_logit, preferred_element_type=jnp.float32),
        ("seq", "hid"),
        scatter_dimension=0,
        tiled=True,
    )
    d_norm = jnp.einsum("fkc,dkc->fkd", d_logit, full_head, preferred_element_type=jnp.float32)
    gated = depth_gain[None] * d_norm
    d_x = scale * gated - x_rows * scale**3 * jnp.mean(gated * x_rows, axis=2, keepdims=True)
    d_round = d_x.astype(jnp.bfloat16)
    d_ratio = jnp.sum(d_x * proj, axis=(1, 2))
    correction = ratio**3 * d_ratio / width_in
    rows_back, ratio_back, corr_back = (
        lax.all_gather(d_round, "hid", axis=0, tiled=True),
        lax.all_gather(ratio.astype(jnp.bfloat16), "hid", axis=0, tiled=True).astype(ratio.dtype),
        lax.all_gather(correction.astype(jnp.bfloat16), "hid", axis=0, tiled=True).astype(
            correction.dtype
        ),
    )
    scaled = (ratio_back[:, None, None] * rows_back.astype(jnp.float32)).astype(jnp.bfloat16)
    in_term = jnp.einsum("fd,fke->kde", hidden, scaled, preferred_element_type=jnp.float32)
    grad_in = lax.psum_scatter(in_term, "seq", scatter_dimension=2, tiled=True)
    back = jnp.einsum("fke,kde->fd", rows_back, w_in, preferred_element_type=jnp.float32)
    grad_hidden = (ratio_back[:, None] * back - corr_back[:, None] * hidden_f).astype(jnp.bfloat16)
    return (grad_hidden, grad_in, grad_out)


def solution(mesh):
    placed = (
        P("seq", "hid"),
        P(None, "hid", None),
        P(),
        P(),
        P(("seq", "hid"), None, None),
        P(None, ("seq", "hid")),
    )
    return jax.shard_map(
        shards,
        mesh=mesh,
        in_specs=placed,
        out_specs=(P("seq", "hid"), P(None, "hid", "seq"), P(("seq", "hid"), None, None)),
        check_vma=False,
    )
```

profile of v0, /device:TPU:1, one launch (start us, length us, event | category | flops | bytes accessed | tf_op | source)
XLA Modules:
  0.0 623.6 jit_solution(17267702258610093383)
XLA Ops:
  8.0 0.0 copy-start
  8.0 0.0 reduce-scatter.7.cloned.1.call-start
  8.1 1.5 copy-done
  9.6 4.3 fusion.7
  13.9 5.4 copy.31
  19.3 0.0 copy-start.4
  19.3 0.0 reduce-scatter.7.cloned.1.call-update
  19.3 0.0 all-gather.3.cloned.1.call-start
  19.4 0.7 copy-done.5
  20.1 0.7 copy.22
  20.8 0.0 all-gather.3.cloned.1.call-update
  20.8 0.0 all-gather.5.cloned.1.call-start
  20.9 0.0 copy-done.7
  20.9 0.6 fusion.16
  22.1 0.0 copy-done.6
  22.2 3.5 gather_fusion
  25.7 0.0 copy-done.3
  25.7 0.2 fusion.5
  25.9 23.2 %all-reduce.3 = f32[512]{0:T(512)S(1)} all-reduce(f32[512]{0:T(512)S(1)} %fusion.5), channel_id=2, replica_groups=mesh['seq'=16,'hid'=8] {'hid'}, use_global_device_ids=true, to_apply=%region_1.0.clone | all-reduce | flops 512 | bytes 4096
  49.0 0.1 fusion.14
  49.1 0.1 bitcast_select_fusion
  49.2 58.5 %reduce-scatter.7.cloned.1.call-done = f32[64,2048]{1,0:T(8,128)} async-done(((f32[512,2048]{1,0:T(8,128)}), f32[64,2048]{1,0:T(8,128)}) %reduce-scatter.7.cloned.1.call-update) | async-done | bytes 524304
  107.7 2.4 copy.32
  110.1 1.5 copy.21
  111.7 0.2 multiply_reduce_fusion.2
  111.9 236.0 %all-gather.3.cloned.1.call-done = bf16[1024,2,2048]{2,0,1:T(8,128)(2,1)} async-done(((bf16[8,2,2048]{2,0,1:T(8,128)(2,1)}), bf16[1024,2,2048]{2,0,1:T(8,128)(2,1)}) %all-gather.3.cloned.1.call-update) | async-done | bytes 8388624 | tf_op jit(solution)/shard_map/all_gather | solution.py:32
  347.9 0.0 copy-done.4
  347.9 5.3 fusion.17
  353.2 0.3 exponential_reduce_fusion
  353.5 0.2 copy-done.1
  353.7 2.8 multiply_reduce_fusion.1
  356.4 0.0 copy-done.2
  356.5 1.0 multiply_reduce_fusion
  357.5 0.0 all-gather.5.cloned.1.call-update
  357.5 0.0 all-reduce.8.cloned.1.call-start
  357.6 9.4 %convolution_bitcast_fusion = f32[1024,2,2048]{0,2,1:T(8,128)} fusion(f32[2,1024]{1,0:T(2,128)S(1)} %copy-done.4, f32[64,2]{0,1:T(2,128)S(1)} %get-tuple-element.16, f32[64,2,2048]{2,0,1:T(8,128)} %copy-done.2, s32[64,2]{0,1:T(2,128)S(1)} %bitcast.45, f32[64,2]{0,1:T(2,128)S(1)} %log_add_fusion, f32[64,2,1024]{2,0,1:T(8,128)S(1)} %copy.21, ...), kind=kOutput, calls=%fused_computation.1 | convolution fusion | flops 539230208 | bytes 18491136 | tf_op jit(solution)/shard_map/fkd,fkc->dkc/dot_general | solution.py:42
  367.0 25.4 %copy.25 = f32[1024,2,2048]{2,1,0:T(2,128)} copy(f32[1024,2,2048]{0,2,1:T(8,128)} %convolution_bitcast_fusion) | data formatting | bytes 33554432 | tf_op jit(solution)/shard_map/fkd,fkc->dkc/transpose | solution.py:42
  392.4 0.0 all-reduce.8.cloned.1.call-update
  392.4 0.0 reduce-scatter.5.cloned.1.call-start
  393.1 0.2 dynamic-update-slice
  393.4 0.2 dynamic-update-slice.1
  393.6 21.0 %all-reduce.5 = (bf16[512]{0:T(512)(128)(2,1)S(1)}, bf16[512]{0:T(512)(128)(2,1)S(1)}) all-reduce(bf16[512]{0:T(512)(128)(2,1)S(1)} %dynamic-update-slice.1, bf16[512]{0:T(512)(128)(2,1)S(1)} %dynamic-update-slice), channel_id=1, replica_groups=mesh['seq'=16,'hid'=8] {'hid'}, use_global_device_ids=true, to_apply=%add.2 | all-reduce | flops 1024 | bytes 4096
  414.6 0.0 all-gather.5.cloned.1.call-done
  414.7 5.2 convolution_bitcast_fusion.2
  419.8 0.0 reduce-scatter.5.cloned.1.call-update
  419.9 3.8 fusion.3
  423.6 191.3 %all-reduce.8.cloned.1.call-done = f32[1024,2,2048]{2,1,0:T(2,128)} async-done(((f32[1024,2,2048]{2,1,0:T(2,128)}), f32[1024,2,2048]{2,1,0:T(2,128)}) %all-reduce.8.cloned.1.call-update) | async-done | bytes 16777232
  615.0 1.6 constant_dynamic-slice_fusion
  (19 shorter events, 0.1 us)
Async XLA Ops:
  8.0 1.6 copy-start
  8.0 99.7 %reduce-scatter.7.cloned.1.call-start = ((), (), s32[]{:S(2)}) async-start(), calls=%async_computation.5 | async-start | bytes 4718592
  19.3 0.8 copy-start.5
  19.3 1.6 copy-start.7
  19.3 2.8 copy-start.6
  19.3 6.4 %copy-start.3 = (bf16[512,512]{1,0:T(8,128)(2,1)S(1)}, bf16[512,512]{1,0:T(8,128)(2,1)}, u32[]{:S(2)}) copy-start(bf16[512,512]{1,0:T(8,128)(2,1)} %param.6) | copy-start | bytes 1572868
  19.3 328.6 %copy-start.4 = (f32[2,1024]{1,0:T(2,128)S(1)}, f32[2,1024]{1,0:T(2,128)}, u32[]{:S(2)}) copy-start(f32[2,1024]{1,0:T(2,128)} %param.9) | copy-start | bytes 24580
  19.3 328.5 %all-gather.3.cloned.1.call-start = ((), (), s32[]{:S(2)}) async-start(), calls=%async_computation.2 | async-start | bytes 8454144 | tf_op jit(solution)/shard_map/all_gather | solution.py:32
  20.8 393.8 %all-gather.5.cloned.1.call-start = ((), (), s32[]{:S(2)}) async-start(), calls=%async_computation.3 | async-start | bytes 2359296 | tf_op jit(solution)/shard_map/all_gather | solution.py:54
  347.9 5.8 copy-start.1
  353.2 3.3 copy-start.2
  357.5 257.4 %all-reduce.8.cloned.1.call-start = ((), (), s32[]{:S(2)}) async-start(), calls=%async_computation.6 | async-start | bytes 33554432
  392.4 224.1 %reduce-scatter.5.cloned.1.call-start = ((), (), s32[]{:S(2)}) async-start(), calls=%async_computation.4 | async-start | bytes 4456448 | tf_op jit(solution)/shard_map/reduce_scatter | solution.py:62
Sparse Core Ops, SparseCore 0:
  19.5 88.1 reduce-scatter.6
  357.6 55.4 all-gather.4
  420.0 69.6 reduce-scatter.4
Sparse Core Ops, SparseCore 1:
  22.1 325.7 all-gather.2
  392.5 222.4 all-reduce.7
where the time goes:
time: 625 us; the launch traced here: 624 us
  waiting for transfers between devices  486 us (78%)
  local copies, waits for them, and re-layouts  44.2 us (7%)
  blocking collectives  44.1 us (7%)
  matrix products  30.7 us (5%)
  between operations  16.6 us (3%)
    unnamed x7, waiting for transfers between devices  250 us
    all_gather x1, waiting for transfers between devices, shards(): full_head = lax.all_gather(w_out, ('seq', 'hid'), axis=0, tiled=True)  236 us
    unnamed x2, blocking collectives  44.1 us
    transpose x1, local copies, waits for them, and re-layouts, shards(): jnp.einsum('fkd,fkc->dkc', normed, d_logit, preferred_element_type=jnp.fl...  25.4 us
    unnamed x25, local copies, waits for them, and re-layouts  13.7 us
  transfers between devices with their start and end apart: 5, of which 3 were waited for; matrix products, arithmetic and copies ran while one was open for 9% of the time, Pallas kernels for 0%

commit v1 on v0

--- a/solution.py
+++ b/solution.py
@@ -29,7 +29,10 @@
     x_rows = ratio[:, None, None] * proj + jnp.stack(pieces, axis=1)
     scale = lax.rsqrt(jnp.mean(x_rows * x_rows, axis=2, keepdims=True) + 1e-06)
     normed = (x_rows * scale * depth_gain[None]).astype(jnp.bfloat16)
-    full_head = lax.all_gather(w_out, ("seq", "hid"), axis=0, tiled=True)
+    full_head = jnp.concatenate(
+        lax.all_to_all(jnp.stack([w_out] * lax.axis_size(("seq", "hid"))), ("seq", "hid"), 0, 0),
+        axis=0,
+    )
     logits = jnp.einsum("fkd,dkc->fkc", normed, full_head, preferred_element_type=jnp.float32)
     targets = codebook_ids.T
     lse = jax.nn.logsumexp(logits, axis=2)

time: 625 us -> 560 us (0.90)
  waiting for transfers between devices: 486 us -> 321 us
  blocking collectives: 44.1 us -> 126 us
  starting transfers between devices: 0.21 us -> 12.1 us
    all_gather x1 -> x0, waiting for transfers between devices: 236 us -> none  [shards(): full_head = lax.all_gather(w_out, ('seq', 'hid'), axis=0, tiled=True)]
    unnamed x2, blocking collectives: 44.1 us -> 126 us
    reduce_scatter x1, waiting for transfers between devices: 0.01 us -> 63.2 us  [shards(): grad_in = lax.psum_scatter(in_term, 'seq', scatter_dimension=2, tiled=True)]
    all_to_all x0 -> x1, starting transfers between devices: none -> 11.9 us  [shards(): lax.all_to_all(jnp.stack([w_out] * lax.axis_size(('seq', 'hid'))), ('seq'...]
    unnamed x7 -> x6, waiting for transfers between devices: 250 us -> 258 us
    unnamed x25 -> x23, local copies, waits for them, and re-layouts: 13.7 us -> 12.8 us
  transfers between devices with their start and end apart: 5 -> 5, of which waited for: 3 -> 3; matrix products, arithmetic and copies ran while one was open for 9% -> 11% of each run, Pallas kernels for 0% -> 0%
where the time goes in v1:
time: 560 us; the launch traced here: 556 us
  waiting for transfers between devices  321 us (57%)
  blocking collectives  126 us (22%)
  local copies, waits for them, and re-layouts  47.6 us (8%)
  matrix products  32.9 us (6%)
  between operations  15.2 us (3%)
  starting transfers between devices  12.1 us (2%)
    unnamed x6, waiting for transfers between devices  258 us
    unnamed x2, blocking collectives  126 us
    reduce_scatter x1, waiting for transfers between devices, shards(): grad_in = lax.psum_scatter(in_term, 'seq', scatter_dimension=2, tiled=True)  63.2 us
    transpose x1, local copies, waits for them, and re-layouts, shards(): jnp.einsum('fkd,fkc->dkc', normed, d_logit, preferred_element_type=jnp.fl...  25.4 us
    unnamed x23, local copies, waits for them, and re-layouts  12.8 us
    all_to_all x1, starting transfers between devices, shards(): lax.all_to_all(jnp.stack([w_out] * lax.axis_size(('seq', 'hid'))), ('seq'...  11.9 us
  transfers between devices with their start and end apart: 5, of which 3 were waited for; matrix products, arithmetic and copies ran while one was open for 11% of the time, Pallas kernels for 0%

profile of v1, /device:TPU:1, one launch (start us, length us, event | category | flops | bytes accessed | tf_op | source)
XLA Modules:
  0.0 556.1 jit_solution(9693335959632997892)
XLA Ops:
  7.2 0.0 copy-start
  7.2 0.0 reduce-scatter.7.cloned.1.call-start
  7.2 1.5 copy-done
  8.8 4.3 fusion.21
  13.0 5.4 copy.32
  18.4 0.0 copy-start.3
  18.4 0.0 reduce-scatter.7.cloned.1.call-update
  18.4 0.8 copy-done.3
  19.3 4.3 stack.8
  23.5 11.9 %all-to-all-start = ((bf16[128,8,2,2048]{3,1,2,0:T(8,128)(2,1)}), bf16[128,8,2,2048]{3,1,2,0:T(8,128)(2,1)}, u32[]{:S(2)}, u32[]{:S(2)}) async-start(bf16[128,8,2,2048]{3,1,2,0:T(8,128)(2,1)} %stack.8), calls=%async_computation | async-start | bytes 16777216 | tf_op jit(solution)/shard_map/all_to_all | solution.py:33
  35.5 0.0 copy-start.4
  35.5 0.0 all-gather.2.cloned.1.call-start
  35.6 0.0 copy-done.6
  35.6 0.6 fusion.30
  36.8 0.0 copy-done.5
  36.9 3.5 gather_fusion
  40.4 0.0 copy-done.1
  40.4 0.2 fusion.19
  40.6 107.6 %all-reduce.3 = f32[512]{0:T(512)S(1)} all-reduce(f32[512]{0:T(512)S(1)} %fusion.19), channel_id=2, replica_groups=mesh['seq'=16,'hid'=8] {'hid'}, use_global_device_ids=true, to_apply=%region_1.0.clone | all-reduce | flops 512 | bytes 4096
  148.2 0.1 fusion.28
  148.3 0.1 bitcast_select_fusion
  148.4 47.2 %reduce-scatter.7.cloned.1.call-done = f32[64,2048]{1,0:T(8,128)} async-done(((f32[512,2048]{1,0:T(8,128)}), f32[64,2048]{1,0:T(8,128)}) %reduce-scatter.7.cloned.1.call-update) | async-done | bytes 524304
  195.5 2.4 copy.33
  197.9 1.5 copy.21
  199.5 0.2 multiply_reduce_fusion.2
  199.7 0.0 all-to-all-done
  199.7 0.0 copy-done.4
  199.7 5.1 fusion.31
  204.9 0.3 exponential_reduce_fusion
  205.2 5.2 multiply_reduce_fusion.1
  210.4 0.0 copy-done.2
  210.4 1.0 multiply_reduce_fusion
  211.5 0.0 all-gather.2.cloned.1.call-update
  211.5 0.0 all-reduce.8.cloned.1.call-start
  211.5 9.4 %convolution_bitcast_fusion = f32[1024,2,2048]{0,2,1:T(8,128)} fusion(f32[2,1024]{1,0:T(2,128)S(1)} %copy-done.4, f32[64,2]{0,1:T(2,128)S(1)} %get-tuple-element.16, f32[64,2,2048]{2,0,1:T(8,128)} %copy-done.2, s32[64,2]{0,1:T(2,128)S(1)} %bitcast.58, f32[64,2]{0,1:T(2,128)S(1)} %log_add_fusion, f32[64,2,1024]{2,0,1:T(8,128)S(1)} %copy.21, ...), kind=kOutput, calls=%fused_computation.7 | convolution fusion | flops 539230208 | bytes 18491136 | tf_op jit(solution)/shard_map/fkd,fkc->dkc/dot_general | solution.py:45
  220.9 25.4 %copy.26 = f32[1024,2,2048]{2,1,0:T(2,128)} copy(f32[1024,2,2048]{0,2,1:T(8,128)} %convolution_bitcast_fusion) | data formatting | bytes 33554432 | tf_op jit(solution)/shard_map/fkd,fkc->dkc/transpose | solution.py:45
  246.4 0.0 all-reduce.8.cloned.1.call-update
  246.4 0.0 reduce-scatter.5.cloned.1.call-start
  247.1 0.2 dynamic-update-slice
  247.4 0.2 dynamic-update-slice.1
  247.6 18.0 %all-reduce.5 = (bf16[512]{0:T(512)(128)(2,1)S(1)}, bf16[512]{0:T(512)(128)(2,1)S(1)}) all-reduce(bf16[512]{0:T(512)(128)(2,1)S(1)} %dynamic-update-slice.1, bf16[512]{0:T(512)(128)(2,1)S(1)} %dynamic-update-slice), channel_id=1, replica_groups=mesh['seq'=16,'hid'=8] {'hid'}, use_global_device_ids=true, to_apply=%add.2 | all-reduce | flops 1024 | bytes 4096
  265.6 0.0 all-gather.2.cloned.1.call-done
  265.6 5.2 convolution_bitcast_fusion.1
  270.8 0.0 reduce-scatter.5.cloned.1.call-update
  270.8 3.7 fusion.12
  274.5 210.4 %all-reduce.8.cloned.1.call-done = f32[1024,2,2048]{2,1,0:T(2,128)} async-done(((f32[1024,2,2048]{2,1,0:T(2,128)}), f32[1024,2,2048]{2,1,0:T(2,128)}) %all-reduce.8.cloned.1.call-update) | async-done | bytes 16777232
  484.8 1.6 constant_dynamic-slice_fusion
  486.4 63.2 %reduce-scatter.5.cloned.1.call-done = f32[2,512,64]{1,2,0:T(8,128)} async-done(((f32[2,512,1024]{1,2,0:T(8,128)}), f32[2,512,64]{1,2,0:T(8,128)}) %reduce-scatter.5.cloned.1.call-update) | async-done | bytes 262160 | tf_op jit(solution)/shard_map/reduce_scatter | solution.py:65
  (17 shorter events, 0.1 us)
Async XLA Ops:
  7.2 1.6 copy-start
  7.2 188.4 %reduce-scatter.7.cloned.1.call-start = ((), (), s32[]{:S(2)}) async-start(), calls=%async_computation.5 | async-start | bytes 4718592
  18.4 0.8 copy-start.3
  23.5 12.0 %copy-start.6 = (u32[128]{0:T(128)S(1)}, u32[128]{0:T(128)}, u32[]{:S(2)}) copy-start(u32[128]{0:T(128)} %constant.44) | copy-start | bytes 1540
  23.5 13.3 %copy-start.5 = (s32[2,64]{1,0:T(2,128)S(1)}, s32[2,64]{1,0:T(2,128)}, u32[]{:S(2)}) copy-start(s32[2,64]{1,0:T(2,128)} %param.11) | copy-start | bytes 1540
  23.5 16.9 %copy-start.1 = (bf16[512,512]{1,0:T(8,128)(2,1)S(1)}, bf16[512,512]{1,0:T(8,128)(2,1)}, u32[]{:S(2)}) copy-start(bf16[512,512]{1,0:T(8,128)(2,1)} %param.6) | copy-start | bytes 1572868
  23.5 176.2 %all-to-all-start = ((bf16[128,8,2,2048]{3,1,2,0:T(8,128)(2,1)}), bf16[128,8,2,2048]{3,1,2,0:T(8,128)(2,1)}, u32[]{:S(2)}, u32[]{:S(2)}) async-start(bf16[128,8,2,2048]{3,1,2,0:T(8,128)(2,1)} %stack.8), calls=%async_computation | async-start | bytes 16777216 | tf_op jit(solution)/shard_map/all_to_all | solution.py:33
  35.5 164.2 %copy-start.4 = (f32[2,1024]{1,0:T(2,128)S(1)}, f32[2,1024]{1,0:T(2,128)}, u32[]{:S(2)}) copy-start(f32[2,1024]{1,0:T(2,128)} %param.9) | copy-start | bytes 24580
  35.5 230.1 %all-gather.2.cloned.1.call-start = ((), (), s32[]{:S(2)}) async-start(), calls=%async_computation.3 | async-start | bytes 2359296 | tf_op jit(solution)/shard_map/all_gather | solution.py:57
  204.8 5.6 %copy-start.2 = (f32[64,2,2048]{2,0,1:T(8,128)}, f32[64,2,2048]{2,0,1:T(8,128)S(1)}, u32[]{:S(2)}) copy-start(f32[64,2,2048]{2,0,1:T(8,128)S(1)} %get-tuple-element.20) | copy-start | bytes 3145732
  211.5 273.4 %all-reduce.8.cloned.1.call-start = ((), (), s32[]{:S(2)}) async-start(), calls=%async_computation.6 | async-start | bytes 33554432
  246.4 303.2 %reduce-scatter.5.cloned.1.call-start = ((), (), s32[]{:S(2)}) async-start(), calls=%async_computation.4 | async-start | bytes 4456448 | tf_op jit(solution)/shard_map/reduce_scatter | solution.py:65
Sparse Core Ops, SparseCore 0:
  18.5 176.9 reduce-scatter.6
  211.6 53.2 all-gather.1
  270.4 214.3 all-reduce.7
  487.7 61.8 reduce-scatter.4
